TPU v7x, 32 devices: a whole 2x2x4 slice. The times are simulated.
32 devices in a mesh: dp: 2 (over y), ep: 16 (over z, x, core).
Axes of the slice: x: 2, y: 2, z: 4, core: 2. Of those that a mesh axis runs over, the one named last changes fastest.
Arguments:
- hidden_in: bfloat16 [768, 4096], P(('dp', 'ep')), may hold values from -6 to 6
- expert_ids: int32 [768, 2], P(('dp', 'ep')), may hold values from 0 to 15, all different within a row; in each aligned block of 24 rows (0 to 23, 24 to 47, ...) at most 4 rows name the same one
- route_logits: float32 [768, 16], P(('dp', 'ep')), may hold values from -10 to 10
- first_weight: bfloat16 [16, 4096, 1024], P('ep', None, 'dp'), may hold values from -0.09375 to 0.09375
- second_weight: bfloat16 [16, 1024, 4096], P('ep', None, 'dp'), may hold values from -0.1875 to 0.1875
- queries: bfloat16 [768, 2048], P(('dp', 'ep')), may hold values from -140 to 140
- span_keys: bfloat16 [768, 2048], P(('dp', 'ep')), may hold values from -7 to 7
- span_values: bfloat16 [768, 2048], P(('dp', 'ep')), may hold values from -6 to 6
- cache_keys: bfloat16 [32, 72, 2048], P(('dp', 'ep')), may hold values from -6 to 6
- cache_values: bfloat16 [32, 72, 2048], P(('dp', 'ep')), may hold values from -6 to 6
- valid_frames: int32 [32], P(('dp', 'ep')), may hold values from 1 to 3
Outputs:
- mixed: bfloat16 [768, 4096], P(('dp', 'ep'))
- attended: bfloat16 [768, 2048], P(('dp', 'ep'))
Inputs may be any that keep to these rules, and one draw needn't show every extreme that they name: `expert_ids`: each token names two different experts. In the rows of one device (24 rows) no expert is named more than 4 times, a bound that some block reaches.
All inputs are finite; a program needn't handle non-finite values.
Results may differ from a plain program's by a relative error of at most 0.0057.
Values may be sent and summed in bfloat16 or wider, within the bound.
A program may use at most 128 MiB of HBM per device.

v0:
```python
import math

import jax
import jax.numpy as jnp
from jax import lax
from jax.sharding import PartitionSpec as P

HEADS = 16
HEAD_DIM = 128
FRAME_TOK = 24


def activate(pre):
    return jax.nn.gelu(pre, approximate=True).astype(jnp.bfloat16)


def expert_slots(expert_ids):
    flat_ids = expert_ids.reshape(-1)
    assigned = flat_ids.shape[0]
    row_ids = lax.broadcasted_iota(jnp.int32, (assigned, assigned), 0)
    col_ids = lax.broadcasted_iota(jnp.int32, (assigned, assigned), 1)
    same_expert = (flat_ids[:, None] == flat_ids[None, :]) & (col_ids < row_ids)
    return jnp.sum(same_expert.astype(jnp.int32), axis=1).reshape(expert_ids.shape)


def attend(queries, span_keys, span_values, cache_keys, cache_values, valid_count):
    token_count = queries.shape[0]
    cache_len = cache_keys.shape[0]
    key_rows = jnp.concatenate([cache_keys, span_keys], axis=0)
    value_rows = jnp.concatenate([cache_values, span_values], axis=0)
    query_heads = queries.reshape(token_count, HEADS, HEAD_DIM)
    key_heads = key_rows.reshape(-1, HEADS, HEAD_DIM)
    value_heads = value_rows.reshape(-1, HEADS, HEAD_DIM)
    scores = jnp.einsum(
        "thd,khd->htk", query_heads, key_heads, preferred_element_type=jnp.float32
    ) * (1.0 / math.sqrt(HEAD_DIM))
    position = lax.broadcasted_iota(jnp.int32, (key_rows.shape[0],), 0)
    usable = (position >= cache_len) | (position // FRAME_TOK < valid_count)
    scores = jnp.where(usable[None, None, :], scores, -1e30)
    row_max = jnp.max(scores, axis=2, keepdims=True)
    weights = jnp.exp(scores - row_max)
    weights = (weights / jnp.sum(weights, axis=2, keepdims=True)).astype(jnp.bfloat16)
    result = jnp.einsum("htk,khd->thd", weights, value_heads, preferred_element_type=jnp.float32)
    return result.astype(jnp.bfloat16).reshape(token_count, HEADS * HEAD_DIM)


def shards(
    hidden_in,
    expert_ids,
    route_logits,
    first_weight,
    second_weight,
    queries,
    span_keys,
    span_values,
    cache_keys,
    cache_values,
    valid_frames,
):
    tokens, model_width = hidden_in.shape
    experts = lax.axis_size("ep")
    capacity = max(2, 8 * tokens // (3 * experts))
    slots = expert_slots(expert_ids)
    places = expert_ids * capacity + slots
    place_ids = lax.broadcasted_iota(jnp.int32, (tokens, experts * capacity), 1)
    picks = [places[:, column : column + 1] == place_ids for column in range(2)]
    chooser = (picks[0] | picks[1]).astype(jnp.bfloat16)
    dispatch = lax.dot_general(
        chooser, hidden_in, (((0,), (0,)), ((), ())), preferred_element_type=jnp.float32
    )
    dispatch = dispatch.astype(jnp.bfloat16).reshape(experts, capacity, model_width)
    expert_cols = lax.broadcasted_iota(jnp.int32, route_logits.shape, 1)
    chosen = jnp.stack(
        [
            jnp.sum(
                jnp.where(expert_cols == expert_ids[:, column : column + 1], route_logits, 0.0),
                axis=1,
            )
            for column in range(2)
        ],
        axis=1,
    )
    gates = jax.nn.softmax(chosen, axis=1)
    first_local = first_weight[0]
    second_local = second_weight[0]
    received = lax.all_to_all(dispatch, "ep", split_axis=0, concat_axis=0, tiled=True)
    sources, item_count, _ = received.shape
    expert_rows = received.reshape(sources * item_count, model_width)
    hidden = activate(
        jnp.dot(
            lax.all_gather(expert_rows, "dp", axis=0, tiled=True),
            first_local,
            preferred_element_type=jnp.float32,
        )
    )
    columns = jnp.dot(
        lax.all_gather(hidden, "dp", axis=1, tiled=True),
        second_local,
        preferred_element_type=jnp.float32,
    ).astype(jnp.bfloat16)
    result = lax.all_to_all(columns, "dp", split_axis=0, concat_axis=1, tiled=True)
    outputs = result.reshape(sources, item_count, model_width)
    returned = lax.all_to_all(outputs, "ep", split_axis=0, concat_axis=0, tiled=True)
    attended = attend(
        queries, span_keys, span_values, cache_keys[0], cache_values[0], valid_frames[0]
    )
    flat_back = returned.reshape(experts * capacity, model_width)
    running = jnp.zeros((tokens, model_width), jnp.float32)
    for column in range(2):
        picked = jnp.dot(
            picks[column].astype(jnp.bfloat16), flat_back, preferred_element_type=jnp.float32
        )
        running = running + gates[:, column : column + 1] * picked
    mixed = running.astype(jnp.bfloat16)
    return (mixed, attended)


def solution(mesh):
    placed = (
        P(("dp", "ep"), None),
        P(("dp", "ep"), None),
        P(("dp", "ep"), None),
        P("ep", None, "dp"),
        P("ep", None, "dp"),
        P(("dp", "ep"), None),
        P(("dp", "ep"), None),
        P(("dp", "ep"), None),
        P(("dp", "ep"), None, None),
        P(("dp", "ep"), None, None),
        P(("dp", "ep")),
    )
    return jax.shard_map(
        shards,
        mesh=mesh,
        in_specs=placed,
        out_specs=(P(("dp", "ep"), None), P(("dp", "ep"), None)),
        check_vma=False,
    )
```

profile of v0, /device:TPU:0, one launch (start us, length us, event | category | flops | bytes accessed | tf_op | source)
XLA Modules:
  0.0 104.6 jit_solution(16428109873670727826)
XLA Ops:
  7.2 0.0 copy-start
  7.2 0.0 copy-start.4
  7.2 0.0 copy-start.5
  7.2 0.0 all-gather.2.cloned.1.call-start
  7.2 0.9 copy.47
  8.1 0.1 eq.61
  8.2 0.2 convert_reduce_fusion
  8.4 0.1 reshape.68
  8.5 0.1 copy.48
  8.6 0.7 multiply_add_fusion
  9.3 0.0 copy-done
  9.3 0.4 convolution_convert_fusion
  9.7 0.2 reshape.69
  9.9 21.5 %all_to_all.26 = bf16[16,4,4096]{2,1,0:T(4,128)(2,1)S(1)} all-to-all(bf16[16,4,4096]{2,1,0:T(4,128)(2,1)S(1)} %reshape.69), channel_id=1, replica_groups=mesh['dp'=2,'ep'=16] {'ep'}, dimensions={0} | all-to-all | bytes 1048576 | tf_op jit(solution)/shard_map/all_to_all | solution.py:86
  31.4 0.9 reshape.70
  32.3 0.0 all-gather.2.cloned.1.call-update
  33.0 0.0 copy-done.4
  33.0 0.0 copy-done.5
  33.0 20.3 %all-gather.2.cloned.1.call-done = bf16[128,4096]{1,0:T(8,128)(2,1)} async-done(((bf16[64,4096]{1,0:T(8,128)(2,1)}), bf16[128,4096]{1,0:T(8,128)(2,1)}) %all-gather.2.cloned.1.call-update) | async-done | bytes 1048592 | tf_op jit(solution)/shard_map/all_gather | solution.py:91
  53.3 0.0 copy-start.1
  53.3 3.4 %fusion.30 = bf16[128,512]{1,0:T(8,128)(2,1)S(1)} fusion(bf16[128,4096]{1,0:T(8,128)(2,1)} %all-gather.2.cloned.1.call-done, bf16[1,4096,512]{2,1,0:T(8,128)(2,1)} %param.14), kind=kOutput, calls=%fused_computation.32 | convolution fusion | flops 537460736 | bytes 5373952 | tf_op jit(solution)/shard_map/dot_general | solution.py:90
  56.7 0.0 copy-start.2
  56.7 0.0 copy-start.3
  56.8 5.9 %all_gather.7 = bf16[128,1024]{1,0:T(8,128)(2,1)S(1)} all-gather(bf16[128,512]{1,0:T(8,128)(2,1)S(1)} %fusion.30), channel_id=1, replica_groups=mesh['dp'=2,'ep'=16] {'dp'}, dimensions={1}, use_global_device_ids=true | all-gather | bytes 393216 | tf_op jit(solution)/shard_map/all_gather | solution.py:97
  62.6 0.0 copy-done.1
  62.6 0.0 copy-start.8
  62.6 1.5 %fusion.7 = bf16[128,2048]{1,0:T(8,128)(2,1)} fusion(bf16[128,1024]{1,0:T(8,128)(2,1)S(1)} %all_gather.7, bf16[1,1024,2048]{2,1,0:T(8,128)(2,1)S(1)} %copy-done.1), kind=kOutput, calls=%fused_computation.10 | convolution fusion | flops 537133056 | bytes 4980736 | tf_op jit(solution)/shard_map/dot_general | solution.py:96
  64.2 3.5 %all-to-all-start.1 = ((bf16[2,64,2048]{2,1,0:T(8,128)(2,1)}), bf16[2,64,2048]{2,1,0:T(8,128)(2,1)S(1)}, u32[]{:S(2)}, u32[]{:S(2)}) async-start(bf16[2,64,2048]{2,1,0:T(8,128)(2,1)} %bitcast.9), calls=%async_computation.1 | async-start | bytes 1048576 | tf_op jit(solution)/shard_map/all_to_all | solution.py:101
  67.6 0.0 copy-start.6
  67.7 0.0 copy-start.7
  67.7 0.0 copy-done.2
  67.7 0.1 copy.50
  67.8 0.0 copy-done.3
  67.9 0.1 copy.52
  68.0 0.0 copy-done.8
  68.0 0.5 fusion.60
  68.5 6.4 %all-to-all-done.1 = bf16[2,64,2048]{2,1,0:T(8,128)(2,1)S(1)} async-done(((bf16[2,64,2048]{2,1,0:T(8,128)(2,1)}), bf16[2,64,2048]{2,1,0:T(8,128)(2,1)S(1)}, u32[]{:S(2)}, u32[]{:S(2)}) %all-to-all-start.1) | async-done | bytes 524320 | tf_op jit(solution)/shard_map/all_to_all | solution.py:101
  74.9 0.5 copy.49
  75.4 1.1 %reshape.71 = bf16[16,4,4096]{2,1,0:T(4,128)(2,1)} reshape(bf16[64,2,2048]{2,1,0:T(2,128)(2,1)S(1)} %copy.49) | data formatting | bytes 1048576 | tf_op jit(solution)/shard_map/reshape | solution.py:102
  76.5 5.6 %all-to-all-start.2 = ((bf16[16,4,4096]{2,1,0:T(4,128)(2,1)}), bf16[16,4,4096]{2,1,0:T(4,128)(2,1)S(1)}, u32[]{:S(2)}, u32[]{:S(2)}) async-start(bf16[16,4,4096]{2,1,0:T(4,128)(2,1)} %reshape.71), calls=%async_computation.2 | async-start | bytes 1048576 | tf_op jit(solution)/shard_map/all_to_all | solution.py:103
  82.1 0.3 fusion.14
  82.4 0.7 copy.75
  83.1 0.0 copy-done.6
  83.1 0.0 copy-done.7
  83.2 13.2 %all-to-all-done.2 = bf16[16,4,4096]{2,1,0:T(4,128)(2,1)S(1)} async-done(((bf16[16,4,4096]{2,1,0:T(4,128)(2,1)}), bf16[16,4,4096]{2,1,0:T(4,128)(2,1)S(1)}, u32[]{:S(2)}, u32[]{:S(2)}) %all-to-all-start.2) | async-done | bytes 524320 | tf_op jit(solution)/shard_map/all_to_all | solution.py:103
  96.4 0.1 reshape.72
  96.5 0.3 convolution_multiply_fusion.1
  96.8 0.9 fusion.2
  (12 shorter events, 0.2 us)
Async XLA Ops:
  7.2 2.1 %copy-start = (bf16[24,4096]{1,0:T(8,128)(2,1)S(1)}, bf16[24,4096]{1,0:T(8,128)(2,1)}, u32[]{:S(2)}) copy-start(bf16[24,4096]{1,0:T(8,128)(2,1)} %param.11) | copy-start | bytes 589828
  7.2 25.8 %copy-start.4 = (bf16[24,2048]{1,0:T(8,128)(2,1)S(1)}, bf16[24,2048]{1,0:T(8,128)(2,1)}, u32[]{:S(2)}) copy-start(bf16[24,2048]{1,0:T(8,128)(2,1)} %param.18) | copy-start | bytes 294916
  7.2 25.8 %copy-start.5 = (bf16[24,2048]{1,0:T(8,128)(2,1)S(1)}, bf16[24,2048]{1,0:T(8,128)(2,1)}, u32[]{:S(2)}) copy-start(bf16[24,2048]{1,0:T(8,128)(2,1)} %param.17) | copy-start | bytes 294916
  7.2 46.1 %all-gather.2.cloned.1.call-start = ((), (), s32[]{:S(2)}) async-start(), calls=%async_computation.3 | async-start | bytes 1572864 | tf_op jit(solution)/shard_map/all_gather | solution.py:91
  53.3 9.3 %copy-start.1 = (bf16[1,1024,2048]{2,1,0:T(8,128)(2,1)S(1)}, bf16[1,1024,2048]{2,1,0:T(8,128)(2,1)}, u32[]{:S(2)}) copy-start(bf16[1,1024,2048]{2,1,0:T(8,128)(2,1)} %param.15) | copy-start | bytes 12582916
  56.7 11.0 %copy-start.2 = (bf16[1,72,2048]{2,1,0:T(8,128)(2,1)S(1)}, bf16[1,72,2048]{2,1,0:T(8,128)(2,1)}, u32[]{:S(2)}) copy-start(bf16[1,72,2048]{2,1,0:T(8,128)(2,1)} %param.20) | copy-start | bytes 884740
  56.7 11.1 %copy-start.3 = (bf16[1,72,2048]{2,1,0:T(8,128)(2,1)S(1)}, bf16[1,72,2048]{2,1,0:T(8,128)(2,1)}, u32[]{:S(2)}) copy-start(bf16[1,72,2048]{2,1,0:T(8,128)(2,1)} %param.19) | copy-start | bytes 884740
  62.6 5.4 %copy-start.8 = (bf16[24,2048]{1,0:T(8,128)(2,1)S(1)}, bf16[24,2048]{1,0:T(8,128)(2,1)}, u32[]{:S(2)}) copy-start(bf16[24,2048]{1,0:T(8,128)(2,1)} %param.16) | copy-start | bytes 294916
  64.2 10.7 %all-to-all-start.1 = ((bf16[2,64,2048]{2,1,0:T(8,128)(2,1)}), bf16[2,64,2048]{2,1,0:T(8,128)(2,1)S(1)}, u32[]{:S(2)}, u32[]{:S(2)}) async-start(bf16[2,64,2048]{2,1,0:T(8,128)(2,1)} %bitcast.9), calls=%async_computation.1 | async-start | bytes 1048576 | tf_op jit(solution)/shard_map/all_to_all | solution.py:101
  67.6 15.4 %copy-start.6 = (s32[24,2]{0,1:T(2,128)S(1)}, s32[24,2]{0,1:T(2,128)}, u32[]{:S(2)}) copy-start(s32[24,2]{0,1:T(2,128)} %param.12) | copy-start | bytes 580
  67.7 15.4 %copy-start.7 = (f32[24,16]{0,1:T(8,128)S(1)}, f32[24,16]{0,1:T(8,128)}, u32[]{:S(2)}) copy-start(f32[24,16]{0,1:T(8,128)} %param.13) | copy-start | bytes 4612
  76.5 19.9 %all-to-all-start.2 = ((bf16[16,4,4096]{2,1,0:T(4,128)(2,1)}), bf16[16,4,4096]{2,1,0:T(4,128)(2,1)S(1)}, u32[]{:S(2)}, u32[]{:S(2)}) async-start(bf16[16,4,4096]{2,1,0:T(4,128)(2,1)} %reshape.71), calls=%async_computation.2 | async-start | bytes 1048576 | tf_op jit(solution)/shard_map/all_to_all | solution.py:103
Sparse Core Ops, SparseCore 0:
  32.4 20.8 all-gather.1
where the time goes:
time: 105 us
  waiting for transfers between devices  39.9 us (38%)
  blocking collectives  27.3 us (26%)
  between operations  14.9 us (14%)
  starting transfers between devices  9.14 us (9%)
  matrix products  7.32 us (7%)
  local copies, waits for them, and re-layouts  5.05 us (5%)
    all_to_all x1, blocking collectives, shards(): lax.all_to_all(dispatch, 'ep', split_axis=0, concat_axis=0, tiled=True)  21.5 us
    all_gather x1, waiting for transfers between devices, shards(): lax.all_gather(expert_rows, 'dp', axis=0, tiled=True)  20.3 us
    all_to_all x1, waiting for transfers between devices, shards(): lax.all_to_all(outputs, 'ep', split_axis=0, concat_axis=0, tiled=True)  13.2 us
    all_to_all x1, waiting for transfers between devices, shards(): lax.all_to_all(columns, 'dp', split_axis=0, concat_axis=1, tiled=True)  6.39 us
    all_gather x1, blocking collectives, shards(): lax.all_gather(hidden, 'dp', axis=1, tiled=True)  5.87 us
    all_to_all x1, starting transfers between devices, shards(): lax.all_to_all(outputs, 'ep', split_axis=0, concat_axis=0, tiled=True)  5.61 us
    all_to_all x1, starting transfers between devices, shards(): lax.all_to_all(columns, 'dp', split_axis=0, concat_axis=1, tiled=True)  3.49 us
    dot_general x1, matrix products, shards(): jnp.dot(lax.all_gather(expert_rows, 'dp', axis=0, tiled=True), first_loca...  3.43 us
  transfers between devices with their start and end apart: 3, of which 3 were waited for; matrix products, arithmetic and copies ran while one was open for 2% of the time, Pallas kernels for 0%

commit v1 on v0

v1 whole, which is shorter than its diff:
```python
import functools
import math

import jax
import jax.numpy as jnp
from jax import lax
from jax.experimental import pallas as pl
from jax.experimental.pallas import tpu as pltpu
from jax.sharding import PartitionSpec as P

HEAD_DIM = 128
FRAME_TOK = 24
TILE = 16
MESH = pl.DeviceIdType.MESH


def iota(shape, axis):
    return lax.broadcasted_iota(jnp.int32, shape, axis)


def as_bf16(mask):
    return jnp.where(mask, 1.0, 0.0).astype(jnp.bfloat16)


def log2(n):
    return n.bit_length() - 1


def flip(me, off, n):
    out = jnp.int32(0)
    bit = 1
    while bit < n:
        one = jnp.int32(bit)
        out = out + one * lax.rem(lax.div(me, one) + lax.div(off, one), jnp.int32(2))
        bit *= 2
    return out


def fold_map(shape, long_axis, group, cap):
    long, tiled = iota(shape, long_axis), iota(shape, 1 - long_axis)
    fold = long >> log2(group * cap)
    source = (long & (group * cap - 1)) >> log2(cap)
    slot = long & (cap - 1)
    return as_bf16(tiled == source * TILE + fold * cap + slot)


def dot(a, b):
    return jnp.dot(a, b, preferred_element_type=jnp.float32)


def drain(view, sem):
    pltpu.make_async_copy(view, view, sem).wait()


def attend(q, k, v, ck, cv, frames, out):
    cache_len = ck.shape[0]
    scale = 1.0 / math.sqrt(HEAD_DIM)
    usable = (iota((1, cache_len), 1) // FRAME_TOK) < frames
    contract = (((1,), (1,)), ((), ()))
    for head in range(q.shape[1] // HEAD_DIM):
        cols = slice(head * HEAD_DIM, (head + 1) * HEAD_DIM)
        query = q[:, cols]
        old = lax.dot_general(query, ck[:, cols], contract, preferred_element_type=jnp.float32)
        new = lax.dot_general(query, k[:, cols], contract, preferred_element_type=jnp.float32)
        old = jnp.where(usable, old * scale, -1e30)
        new = new * scale
        top = jnp.maximum(
            jnp.max(old, axis=1, keepdims=True), jnp.max(new, axis=1, keepdims=True)
        )
        old = jnp.exp(old - top)
        new = jnp.exp(new - top)
        total = jnp.sum(old, axis=1, keepdims=True) + jnp.sum(new, axis=1, keepdims=True)
        old = (old / total).astype(jnp.bfloat16)
        new = (new / total).astype(jnp.bfloat16)
        out[:, cols] = (dot(old, cv[:, cols]) + dot(new, v[:, cols])).astype(jnp.bfloat16)


def kernel(
    dp_n, ep_n, cap, back_folds,
    ids, logits, frames, hidden,
    q_hbm, k_hbm, v_hbm, ck_hbm, cv_hbm, w1_hbm, w2_hbm,
    mixed, attended,
    w1, w2, q, k, v, ck, cv,
    disp, rows, xs, hid, ys, back_out, back_in,
    load_sem, disp_send, disp_recv, relay_send, relay_recv,
    hid_send, hid_recv, back_send, back_recv, own_sem,
):
    d, me = lax.axis_index("dp"), lax.axis_index("ep")
    tokens = hidden.shape[0]
    folds = TILE // cap
    fold_cols = disp.shape[2]
    back_cols = back_in.shape[2]
    group = min(ep_n, 16)
    group_rows = group * cap
    total = dp_n * ep_n

    barrier = pltpu.get_barrier_semaphore()

    def greet(i, carry):
        other = lax.rem(d * ep_n + me + i, jnp.int32(total))
        pl.semaphore_signal(
            barrier,
            inc=1,
            device_id={
                "dp": lax.div(other, jnp.int32(ep_n)),
                "ep": lax.rem(other, jnp.int32(ep_n)),
            },
            device_id_type=MESH,
        )
        return carry

    lax.fori_loop(1, total, greet, 0)

    loads = [
        pltpu.make_async_copy(src, dst, load_sem.at[i])
        for i, (src, dst) in enumerate(
            [(w1_hbm, w1), (w2_hbm, w2), (q_hbm, q), (k_hbm, k), (v_hbm, v), (ck_hbm, ck), (cv_hbm, cv)]
        )
    ]
    for load in loads:
        load.start()

    experts = iota((tokens, ep_n), 1)
    named = [experts == ids[:, c : c + 1] for c in range(2)]
    count = as_bf16(named[0] | named[1])
    earlier = as_bf16(iota((tokens, tokens), 1) < iota((tokens, tokens), 0))
    before = dot(earlier, count)
    place, place_row, chosen = [], [], []
    eye = iota((tokens, tokens), 0) == iota((tokens, tokens), 1)
    for c in range(2):
        slot = jnp.sum(jnp.where(named[c], before, 0.0), axis=1, keepdims=True).astype(jnp.int32)
        place.append(ids[:, c : c + 1] * TILE + slot)
        place_row.append(jnp.sum(jnp.where(eye, place[c], 0), axis=0, keepdims=True))
        chosen.append(jnp.sum(jnp.where(named[c], logits[...], 0.0), axis=1, keepdims=True))
    top = jnp.maximum(chosen[0], chosen[1])
    powers = [jnp.exp(x - top) for x in chosen]
    gates = [p / (powers[0] + powers[1]) for p in powers]

    row_at = iota((ep_n * TILE, tokens), 0)
    pickers = [
        as_bf16((row_at - f * cap == place_row[0]) | (row_at - f * cap == place_row[1]))
        for f in range(folds)
    ]
    step = min(fold_cols, 256)
    for at in range(0, fold_cols, step):
        acc = dot(pickers[0], hidden[:, at : at + step])
        for f in range(1, folds):
            acc += dot(pickers[f], hidden[:, f * fold_cols + at : f * fold_cols + at + step])
        disp[:, :, at : at + step] = acc.astype(jnp.bfloat16).reshape(ep_n, TILE, step)

    pl.semaphore_wait(barrier, total - 1)

    def dispatch(i, carry):
        target = flip(me, ep_n - 1 - i, ep_n)
        pltpu.make_async_remote_copy(
            src_ref=disp.at[target],
            dst_ref=rows.at[d * ep_n + me],
            send_sem=disp_send,
            recv_sem=disp_recv.at[me],
            device_id={"dp": d, "ep": target},
            device_id_type=MESH,
        ).start()
        return carry

    lax.fori_loop(0, ep_n - 1, dispatch, 0)
    pltpu.make_async_copy(disp.at[me], rows.at[d * ep_n + me], disp_recv.at[me]).start()

    def relay(off):
        source = flip(me, off, ep_n)
        chunk = rows.at[d * ep_n + source]
        drain(chunk, disp_recv.at[source])
        for j in range(1, dp_n):
            pltpu.make_async_remote_copy(
                src_ref=chunk,
                dst_ref=chunk,
                send_sem=relay_send,
                recv_sem=relay_recv.at[d],
                device_id={"dp": lax.rem(d + j, jnp.int32(dp_n)), "ep": me},
                device_id_type=MESH,
            ).start()

    near = min(4, ep_n)

    def relay_near(i, carry):
        relay(i)
        return carry

    def relay_far(i, carry):
        relay(ep_n - 1 + near - i)
        return carry

    lax.fori_loop(0, near, relay_near, 0)
    lax.fori_loop(near, ep_n, relay_far, 0)

    unfold = fold_map((folds * group_rows, group * TILE), 0, group, cap)
    refold = fold_map((group * TILE, back_folds * group_rows), 1, group, cap)

    loads[0].wait()
    loads[1].wait()
    for j in range(dp_n):
        plane = lax.rem(d + j, jnp.int32(dp_n))
        if j > 0:
            drain(rows.at[pl.ds(plane * ep_n, ep_n)], relay_recv.at[plane])
        for g in range(ep_n // group):
            tiles = rows[pl.ds(plane * ep_n + g * group, group)].reshape(group * TILE, fold_cols)
            flat = dot(unfold, tiles).astype(jnp.bfloat16)
            for f in range(folds):
                xs[f, g * group_rows : (g + 1) * group_rows, :] = flat[
                    f * group_rows : (f + 1) * group_rows
                ]
        acc = dot(xs[0], w1[:fold_cols, :])
        for f in range(1, folds):
            acc += dot(xs[f], w1[f * fold_cols : (f + 1) * fold_cols, :])
        hid[plane * dp_n + d] = jax.nn.gelu(acc, approximate=True).astype(jnp.bfloat16)
        for i in range(1, dp_n):
            pltpu.make_async_remote_copy(
                src_ref=hid.at[plane * dp_n + d],
                dst_ref=hid.at[plane * dp_n + d],
                send_sem=hid_send,
                recv_sem=hid_recv.at[plane * dp_n + d],
                device_id={"dp": lax.rem(d + i, jnp.int32(dp_n)), "ep": me},
                device_id_type=MESH,
            ).start()

    units = hid.shape[2]
    for j in range(dp_n):
        plane = lax.rem(d + j, jnp.int32(dp_n))
        for i in range(1, dp_n):
            part = plane * dp_n + lax.rem(d + i, jnp.int32(dp_n))
            drain(hid.at[part], hid_recv.at[part])
        for f in range(back_folds):
            cols = slice(f * back_cols, (f + 1) * back_cols)
            acc = dot(hid[plane * dp_n], w2[:units, cols])
            for i in range(1, dp_n):
                acc += dot(hid[plane * dp_n + i], w2[i * units : (i + 1) * units, cols])
            ys[f] = acc.astype(jnp.bfloat16)
        for g in range(ep_n // group):
            flat = jnp.concatenate(
                [ys[f, g * group_rows : (g + 1) * group_rows, :] for f in range(back_folds)], axis=0
            )
            tiles = dot(refold, flat).astype(jnp.bfloat16)
            back_out[pl.ds(plane * ep_n + g * group, group)] = tiles.reshape(group, TILE, back_cols)

        def give_back(i, carry):
            target = flip(me, ep_n - 1 - i, ep_n)
            pltpu.make_async_remote_copy(
                src_ref=back_out.at[plane * ep_n + target],
                dst_ref=back_in.at[d * ep_n + me],
                send_sem=back_send,
                recv_sem=back_recv,
                device_id={"dp": plane, "ep": target},
                device_id_type=MESH,
            ).start()
            return carry

        lax.fori_loop(0, ep_n - 1 if j == 0 else ep_n, give_back, 0)
        if j == 0:
            pltpu.make_async_copy(
                back_out.at[d * ep_n + me], back_in.at[d * ep_n + me], own_sem
            ).start()

    for load in loads[2:]:
        load.wait()
    attend(q, k, v, ck, cv, frames[0], attended)

    col_at = iota((tokens, ep_n * TILE), 1)
    picks = jnp.concatenate(
        [
            jnp.where(col_at - f * cap == place[c], 1.0, 0.0)
            for f in range(back_folds)
            for c in range(2)
        ],
        axis=0,
    ).astype(jnp.bfloat16)

    drain(back_in.at[pl.ds(0, total - 1)], back_recv)
    drain(back_in.at[0], own_sem)
    for h in range(dp_n):
        tiles = back_in[h * ep_n : (h + 1) * ep_n].reshape(ep_n * TILE, back_cols)
        picked = dot(picks, tiles)
        for f in range(back_folds):
            at = 2 * f * tokens
            cols = slice((h * back_folds + f) * back_cols, (h * back_folds + f + 1) * back_cols)
            mixed[:, cols] = (
                gates[0] * picked[at : at + tokens] + gates[1] * picked[at + tokens : at + 2 * tokens]
            ).astype(jnp.bfloat16)

    drain(disp.at[pl.ds(0, ep_n - 1)], disp_send)
    if dp_n > 1:
        drain(rows.at[pl.ds(0, (dp_n - 1) * ep_n)], relay_send)
        drain(hid.at[pl.ds(0, dp_n * (dp_n - 1))], hid_send)
    drain(back_out.at[pl.ds(0, total - 1)], back_send)


def shards(dp_n, ep_n, *args):
    (hidden_in, expert_ids, route_logits, first_weight, second_weight,
     queries, span_keys, span_values, cache_keys, cache_values, valid_frames) = args
    tokens, width = hidden_in.shape
    cap = max(2, 8 * tokens // (3 * ep_n))
    _, _, units = first_weight.shape
    _, all_units, cols = second_weight.shape
    folds = TILE // cap
    back_folds = min(folds, cols // 128)
    slots = ep_n * cap
    bf16 = jnp.bfloat16
    vmem, hbm = pl.BlockSpec(memory_space=pltpu.VMEM), pl.BlockSpec(memory_space=pl.ANY)
    dma = pltpu.SemaphoreType.DMA
    total = dp_n * ep_n
    return pl.pallas_call(
        functools.partial(kernel, dp_n, ep_n, cap, back_folds),
        out_shape=(
            jax.ShapeDtypeStruct((tokens, width), bf16),
            jax.ShapeDtypeStruct(queries.shape, bf16),
        ),
        in_specs=[vmem, vmem, pl.BlockSpec(memory_space=pltpu.SMEM), vmem] + [hbm] * 7,
        out_specs=(vmem, vmem),
        scratch_shapes=[
            pltpu.VMEM((width, units), bf16),
            pltpu.VMEM((all_units, cols), bf16),
            pltpu.VMEM(queries.shape, bf16),
            pltpu.VMEM(span_keys.shape, bf16),
            pltpu.VMEM(span_values.shape, bf16),
            pltpu.VMEM(cache_keys.shape[1:], bf16),
            pltpu.VMEM(cache_values.shape[1:], bf16),
            pltpu.VMEM((ep_n, TILE, width // folds), bf16),
            pltpu.VMEM((total, TILE, width // folds), bf16),
            pltpu.VMEM((folds, slots, width // folds), bf16),
            pltpu.VMEM((dp_n * dp_n, slots, units), bf16),
            pltpu.VMEM((back_folds, slots, cols // back_folds), bf16),
            pltpu.VMEM((total, TILE, cols // back_folds), bf16),
            pltpu.VMEM((total, TILE, cols // back_folds), bf16),
            dma((7,)),
            dma(()),
            dma((ep_n,)),
            dma(()),
            dma((dp_n,)),
            dma(()),
            dma((dp_n * dp_n,)),
            dma(()),
            dma(()),
            dma(()),
        ],
        compiler_params=pltpu.CompilerParams(
            collective_id=0, has_side_effects=True, vmem_limit_bytes=60 * 1024 * 1024
        ),
    )(
        expert_ids, route_logits, valid_frames, hidden_in,
        queries, span_keys, span_values, cache_keys[0], cache_values[0],
        first_weight[0], second_weight[0],
    )


def solution(mesh):
    tokens = P(("dp", "ep"), None)
    weights = P("ep", None, "dp")
    cache = P(("dp", "ep"), None, None)
    return jax.shard_map(
        functools.partial(shards, mesh.shape["dp"], mesh.shape["ep"]),
        mesh=mesh,
        in_specs=(
            tokens, tokens, tokens, weights, weights, tokens, tokens, tokens, cache, cache,
            P(("dp", "ep")),
        ),
        out_specs=(tokens, tokens),
        check_vma=False,
    )
```

time: 105 us -> 53.2 us (0.51)
  Pallas kernels: 0 us -> 45.7 us
  waiting for transfers between devices: 39.9 us -> 0 us
  blocking collectives: 27.3 us -> 0 us
  between operations: 14.9 us -> 1.29 us
  starting transfers between devices: 9.14 us -> 0 us
  matrix products: 7.32 us -> 0 us
    pallas_call x0 -> x1, Pallas kernels: none -> 45.7 us  [shards(): pl.pallas_call(functools.partial(kernel, dp_n, ep_n, cap, back_folds), ou...]
    all_to_all x1 -> x0, blocking collectives: 21.5 us -> none  [shards(): lax.all_to_all(dispatch, 'ep', split_axis=0, concat_axis=0, tiled=True)]
    all_gather x1 -> x0, waiting for transfers between devices: 20.3 us -> none  [shards(): lax.all_gather(expert_rows, 'dp', axis=0, tiled=True)]
    all_to_all x2 -> x0, waiting for transfers between devices: 19.6 us -> none  [the longest x1 13.2 us: shards(): lax.all_to_all(outputs, 'ep', split_axis=0, concat_axis=0, tiled=True)]
    all_to_all x2 -> x0, starting transfers between devices: 9.1 us -> none  [the longest x1 5.61 us: shards(): lax.all_to_all(outputs, 'ep', split_axis=0, concat_axis=0, tiled=True)]
    dot_general x6 -> x0, matrix products: 6.84 us -> none  [the longest x1 3.43 us: shards(): jnp.dot(lax.all_gather(expert_rows, 'dp', axis=0, tiled=True), first_loca...]
    all_gather x1 -> x0, blocking collectives: 5.87 us -> none  [shards(): lax.all_gather(hidden, 'dp', axis=1, tiled=True)]
    unnamed x21 -> x4, local copies, waits for them, and re-layouts: 1 us -> 5.88 us
  transfers between devices with their start and end apart: 3 -> 0, of which waited for: 3 -> 0; matrix products, arithmetic and copies ran while one was open for 2% -> 0% of each run, Pallas kernels for 0% -> 0%
where the time goes in v1:
time: 53.2 us; the launch traced here: 52.9 us
  Pallas kernels  45.7 us (86%)
  local copies, waits for them, and re-layouts  5.88 us (11%)
  between operations  1.29 us (2%)
    pallas_call x1, Pallas kernels, shards(): pl.pallas_call(functools.partial(kernel, dp_n, ep_n, cap, back_folds), ou...  45.7 us
    unnamed x4, local copies, waits for them, and re-layouts  5.88 us

profile of v1, /device:TPU:0, one launch (start us, length us, event | category | flops | bytes accessed | tf_op | source)
XLA Modules:
  0.0 52.9 jit_solution(10352839527616042673)
XLA Ops:
  1.3 1.4 %copy.13.ids = s32[24,2]{1,0:T(8,128)} copy(s32[24,2]{0,1:T(2,128)} %param.12) | data formatting | bytes 384 | tf_op args[1]
  2.6 1.4 %copy.14.logits = f32[24,16]{1,0:T(8,128)} copy(f32[24,16]{0,1:T(8,128)} %param.13) | data formatting | bytes 3072 | tf_op args[2]
  4.0 45.7 %shard_map.122 = (bf16[24,4096]{1,0:T(8,128)(2,1)}, bf16[24,2048]{1,0:T(8,128)(2,1)}) custom-call(s32[24,2]{1,0:T(8,128)} %copy.13.ids, f32[24,16]{1,0:T(8,128)} %copy.14.logits, s32[1]{0:T(128)S(6)} %copy.17.frames, bf16[24,4096]{1,0:T(8,128)(2,1)} %hidden.1, bf16[24,2048]{1,0:T(8,128)(2,1)} %q_hbm.1, bf16[24,2048]{1,0:T(8,128)(2,1)} %k_hbm.1, ...), custom_call_target="tpu_custom_call" | custom-call | tf_op jit(solution)/shard_map/pallas_call | solution.py:309
  49.7 1.6 %copy.18 = bf16[24,4096]{1,0:T(8,128)(2,1)} copy(bf16[24,4096]{1,0:T(8,128)(2,1)} %get-tuple-element.4) | data formatting | bytes 393216
  51.4 1.5 %copy.19 = bf16[24,2048]{1,0:T(8,128)(2,1)} copy(bf16[24,2048]{1,0:T(8,128)(2,1)} %get-tuple-element.5) | data formatting | bytes 196608

commit v2 on v1

--- a/solution.py
+++ b/solution.py
@@ -77,10 +77,10 @@
 
 def kernel(
     dp_n, ep_n, cap, back_folds,
-    ids, logits, frames, hidden,
+    frames, ids_hbm, logits_hbm, hidden_hbm,
     q_hbm, k_hbm, v_hbm, ck_hbm, cv_hbm, w1_hbm, w2_hbm,
     mixed, attended,
-    w1, w2, q, k, v, ck, cv,
+    ids, logits, hidden, w1, w2, q, k, v, ck, cv,
     disp, rows, xs, hid, ys, back_out, back_in,
     load_sem, disp_send, disp_recv, relay_send, relay_recv,
     hid_send, hid_recv, back_send, back_recv, own_sem,
@@ -97,44 +97,53 @@
     barrier = pltpu.get_barrier_semaphore()
 
     def greet(i, carry):
-        other = lax.rem(d * ep_n + me + i, jnp.int32(total))
+        pl.semaphore_signal(
+            barrier, inc=1, device_id={"dp": d, "ep": flip(me, i, ep_n)}, device_id_type=MESH
+        )
+        return carry
+
+    lax.fori_loop(1, ep_n, greet, 0)
+    for i in range(1, dp_n):
         pl.semaphore_signal(
             barrier,
             inc=1,
-            device_id={
-                "dp": lax.div(other, jnp.int32(ep_n)),
-                "ep": lax.rem(other, jnp.int32(ep_n)),
-            },
+            device_id={"dp": lax.rem(d + i, jnp.int32(dp_n)), "ep": me},
             device_id_type=MESH,
         )
-        return carry
-
-    lax.fori_loop(1, total, greet, 0)
 
     loads = [
         pltpu.make_async_copy(src, dst, load_sem.at[i])
         for i, (src, dst) in enumerate(
-            [(w1_hbm, w1), (w2_hbm, w2), (q_hbm, q), (k_hbm, k), (v_hbm, v), (ck_hbm, ck), (cv_hbm, cv)]
+            [
+                (ids_hbm, ids), (logits_hbm, logits), (hidden_hbm, hidden),
+                (w1_hbm, w1), (w2_hbm, w2),
+                (q_hbm, q), (k_hbm, k), (v_hbm, v), (ck_hbm, ck), (cv_hbm, cv),
+            ]
         )
     ]
     for load in loads:
         load.start()
-
-    experts = iota((tokens, ep_n), 1)
-    named = [experts == ids[:, c : c + 1] for c in range(2)]
+    for load in loads[:3]:
+        load.wait()
+
+    experts = iota((ep_n, tokens), 0)
+    named = [experts == ids[c : c + 1, :] for c in range(2)]
     count = as_bf16(named[0] | named[1])
-    earlier = as_bf16(iota((tokens, tokens), 1) < iota((tokens, tokens), 0))
-    before = dot(earlier, count)
+    earlier = as_bf16(iota((tokens, tokens), 0) < iota((tokens, tokens), 1))
+    before = dot(count, earlier)
+    eye = iota((tokens, tokens), 0) == iota((tokens, tokens), 1)
     place, place_row, chosen = [], [], []
-    eye = iota((tokens, tokens), 0) == iota((tokens, tokens), 1)
     for c in range(2):
-        slot = jnp.sum(jnp.where(named[c], before, 0.0), axis=1, keepdims=True).astype(jnp.int32)
-        place.append(ids[:, c : c + 1] * TILE + slot)
-        place_row.append(jnp.sum(jnp.where(eye, place[c], 0), axis=0, keepdims=True))
-        chosen.append(jnp.sum(jnp.where(named[c], logits[...], 0.0), axis=1, keepdims=True))
+        slot = jnp.sum(jnp.where(named[c], before, 0.0), axis=0, keepdims=True).astype(jnp.int32)
+        place_row.append(ids[c : c + 1, :] * TILE + slot)
+        place.append(jnp.sum(jnp.where(eye, place_row[c], 0), axis=1, keepdims=True))
+        chosen.append(jnp.sum(jnp.where(named[c], logits[...], 0.0), axis=0, keepdims=True))
     top = jnp.maximum(chosen[0], chosen[1])
     powers = [jnp.exp(x - top) for x in chosen]
-    gates = [p / (powers[0] + powers[1]) for p in powers]
+    gates = [
+        jnp.sum(jnp.where(eye, p / (powers[0] + powers[1]), 0.0), axis=1, keepdims=True)
+        for p in powers
+    ]
 
     row_at = iota((ep_n * TILE, tokens), 0)
     pickers = [
@@ -148,10 +157,10 @@
             acc += dot(pickers[f], hidden[:, f * fold_cols + at : f * fold_cols + at + step])
         disp[:, :, at : at + step] = acc.astype(jnp.bfloat16).reshape(ep_n, TILE, step)
 
-    pl.semaphore_wait(barrier, total - 1)
-
-    def dispatch(i, carry):
-        target = flip(me, ep_n - 1 - i, ep_n)
+    pl.semaphore_wait(barrier, ep_n + dp_n - 2)
+
+    def dispatch(off, carry):
+        target = flip(me, off, ep_n)
         pltpu.make_async_remote_copy(
             src_ref=disp.at[target],
             dst_ref=rows.at[d * ep_n + me],
@@ -162,10 +171,10 @@
         ).start()
         return carry
 
-    lax.fori_loop(0, ep_n - 1, dispatch, 0)
+    lax.fori_loop(1, ep_n, dispatch, 0)
     pltpu.make_async_copy(disp.at[me], rows.at[d * ep_n + me], disp_recv.at[me]).start()
 
-    def relay(off):
+    def relay(off, carry):
         source = flip(me, off, ep_n)
         chunk = rows.at[d * ep_n + source]
         drain(chunk, disp_recv.at[source])
@@ -178,25 +187,15 @@
                 device_id={"dp": lax.rem(d + j, jnp.int32(dp_n)), "ep": me},
                 device_id_type=MESH,
             ).start()
-
-    near = min(4, ep_n)
-
-    def relay_near(i, carry):
-        relay(i)
         return carry
 
-    def relay_far(i, carry):
-        relay(ep_n - 1 + near - i)
-        return carry
-
-    lax.fori_loop(0, near, relay_near, 0)
-    lax.fori_loop(near, ep_n, relay_far, 0)
+    lax.fori_loop(0, ep_n, relay, 0)
 
     unfold = fold_map((folds * group_rows, group * TILE), 0, group, cap)
     refold = fold_map((group * TILE, back_folds * group_rows), 1, group, cap)
 
-    loads[0].wait()
-    loads[1].wait()
+    loads[3].wait()
+    loads[4].wait()
     for j in range(dp_n):
         plane = lax.rem(d + j, jnp.int32(dp_n))
         if j > 0:
@@ -241,8 +240,8 @@
             tiles = dot(refold, flat).astype(jnp.bfloat16)
             back_out[pl.ds(plane * ep_n + g * group, group)] = tiles.reshape(group, TILE, back_cols)
 
-        def give_back(i, carry):
-            target = flip(me, ep_n - 1 - i, ep_n)
+        def give_back(off, carry):
+            target = flip(me, off, ep_n)
             pltpu.make_async_remote_copy(
                 src_ref=back_out.at[plane * ep_n + target],
                 dst_ref=back_in.at[d * ep_n + me],
@@ -253,13 +252,13 @@
             ).start()
             return carry
 
-        lax.fori_loop(0, ep_n - 1 if j == 0 else ep_n, give_back, 0)
+        lax.fori_loop(1 if j == 0 else 0, ep_n, give_back, 0)
         if j == 0:
             pltpu.make_async_copy(
                 back_out.at[d * ep_n + me], back_in.at[d * ep_n + me], own_sem
             ).start()
 
-    for load in loads[2:]:
+    for load in loads[5:]:
         load.wait()
     attend(q, k, v, ck, cv, frames[0], attended)
 
@@ -303,18 +302,26 @@
     back_folds = min(folds, cols // 128)
     slots = ep_n * cap
     bf16 = jnp.bfloat16
-    vmem, hbm = pl.BlockSpec(memory_space=pltpu.VMEM), pl.BlockSpec(memory_space=pl.ANY)
+    vmem, hbm = pl.BlockSpec(memory_space=pltpu.VMEM), pl.BlockSpec(memory_space=pltpu.HBM)
     dma = pltpu.SemaphoreType.DMA
     total = dp_n * ep_n
+    streamed = (
+        expert_ids.T, route_logits.T, hidden_in,
+        queries, span_keys, span_values, cache_keys[0], cache_values[0],
+        first_weight[0], second_weight[0],
+    )
     return pl.pallas_call(
         functools.partial(kernel, dp_n, ep_n, cap, back_folds),
         out_shape=(
             jax.ShapeDtypeStruct((tokens, width), bf16),
             jax.ShapeDtypeStruct(queries.shape, bf16),
         ),
-        in_specs=[vmem, vmem, pl.BlockSpec(memory_space=pltpu.SMEM), vmem] + [hbm] * 7,
+        in_specs=[pl.BlockSpec(memory_space=pltpu.SMEM)] + [hbm] * len(streamed),
         out_specs=(vmem, vmem),
         scratch_shapes=[
+            pltpu.VMEM((2, tokens), jnp.int32),
+            pltpu.VMEM((ep_n, tokens), jnp.float32),
+            pltpu.VMEM((tokens, width), bf16),
             pltpu.VMEM((width, units), bf16),
             pltpu.VMEM((all_units, cols), bf16),
             pltpu.VMEM(queries.shape, bf16),
@@ -329,7 +336,7 @@
             pltpu.VMEM((back_folds, slots, cols // back_folds), bf16),
             pltpu.VMEM((total, TILE, cols // back_folds), bf16),
             pltpu.VMEM((total, TILE, cols // back_folds), bf16),
-            dma((7,)),
+            dma((len(streamed),)),
             dma(()),
             dma((ep_n,)),
             dma(()),
@@ -341,12 +348,11 @@
             dma(()),
         ],
         compiler_params=pltpu.CompilerParams(
-            collective_id=0, has_side_effects=True, vmem_limit_bytes=60 * 1024 * 1024
+            collective_id=0, has_side_effects=True, vmem_limit_bytes=40 * 1024 * 1024
         ),
     )(
-        expert_ids, route_logits, valid_frames, hidden_in,
-        queries, span_keys, span_values, cache_keys[0], cache_values[0],
-        first_weight[0], second_weight[0],
+        valid_frames,
+        *[pltpu.with_memory_space_constraint(x, pltpu.HBM) for x in streamed],
     )
 
 

time: 53.2 us -> 43.6 us (0.82)
  Pallas kernels: 45.7 us -> 40.8 us
  local copies, waits for them, and re-layouts: 5.88 us -> 1.32 us
    pallas_call x1, Pallas kernels: 45.7 us -> 40.8 us  [shards(): pl.pallas_call(functools.partial(kernel, dp_n, ep_n, cap, back_folds), ou...]
    unnamed x4 -> x2, local copies, waits for them, and re-layouts: 5.88 us -> 1.32 us
where the time goes in v2:
time: 43.6 us; the launch traced here: 43.4 us
  Pallas kernels  40.8 us (94%)
  local copies, waits for them, and re-layouts  1.32 us (3%)
  between operations  1.29 us (3%)
    pallas_call x1, Pallas kernels, shards(): pl.pallas_call(functools.partial(kernel, dp_n, ep_n, cap, back_folds), ou...  40.8 us
    unnamed x2, local copies, waits for them, and re-layouts  1.32 us

profile of v2, /device:TPU:0, one launch (start us, length us, event | category | flops | bytes accessed | tf_op | source)
XLA Modules:
  0.0 43.4 jit_solution(10955489604538892622)
XLA Ops:
  1.3 40.8 %shard_map.122 = (bf16[24,4096]{1,0:T(8,128)(2,1)S(1)}, bf16[24,2048]{1,0:T(8,128)(2,1)S(1)}) custom-call(s32[1]{0:T(128)S(6)} %copy.15.frames, s32[2,24]{1,0:T(2,128)} %bitcast.11, f32[16,24]{1,0:T(8,128)} %bitcast.10, bf16[24,4096]{1,0:T(8,128)(2,1)} %hidden_hbm.1, bf16[24,2048]{1,0:T(8,128)(2,1)} %q_hbm.1, bf16[24,2048]{1,0:T(8,128)(2,1)} %k_hbm.1, ...), custom_call_target="tpu_custom_call" | custom-call | tf_op jit(solution)/shard_map/pallas_call | solution.py:313
  42.1 0.7 %copy.16 = bf16[24,4096]{1,0:T(8,128)(2,1)} copy(bf16[24,4096]{1,0:T(8,128)(2,1)S(1)} %get-tuple-element.4) | data formatting | bytes 393216
  42.8 0.6 %copy.17 = bf16[24,2048]{1,0:T(8,128)(2,1)} copy(bf16[24,2048]{1,0:T(8,128)(2,1)S(1)} %get-tuple-element.5) | data formatting | bytes 196608

commit v3 on v2

--- a/solution.py
+++ b/solution.py
@@ -76,7 +76,7 @@
 
 
 def kernel(
-    dp_n, ep_n, cap, back_folds,
+    dp_n, ep_n, passes, cap, back_folds,
     frames, ids_hbm, logits_hbm, hidden_hbm,
     q_hbm, k_hbm, v_hbm, ck_hbm, cv_hbm, w1_hbm, w2_hbm,
     mixed, attended,
@@ -135,7 +135,8 @@
     place, place_row, chosen = [], [], []
     for c in range(2):
         slot = jnp.sum(jnp.where(named[c], before, 0.0), axis=0, keepdims=True).astype(jnp.int32)
-        place_row.append(ids[c : c + 1, :] * TILE + slot)
+        turn = slot >> log2(cap)
+        place_row.append((turn * ep_n + ids[c : c + 1, :]) * TILE + (slot & (cap - 1)))
         place.append(jnp.sum(jnp.where(eye, place_row[c], 0), axis=1, keepdims=True))
         chosen.append(jnp.sum(jnp.where(named[c], logits[...], 0.0), axis=0, keepdims=True))
     top = jnp.maximum(chosen[0], chosen[1])
@@ -145,7 +146,7 @@
         for p in powers
     ]
 
-    row_at = iota((ep_n * TILE, tokens), 0)
+    row_at = iota((passes * ep_n * TILE, tokens), 0)
     pickers = [
         as_bf16((row_at - f * cap == place_row[0]) | (row_at - f * cap == place_row[1]))
         for f in range(folds)
@@ -155,53 +156,58 @@
         acc = dot(pickers[0], hidden[:, at : at + step])
         for f in range(1, folds):
             acc += dot(pickers[f], hidden[:, f * fold_cols + at : f * fold_cols + at + step])
-        disp[:, :, at : at + step] = acc.astype(jnp.bfloat16).reshape(ep_n, TILE, step)
+        disp[:, :, at : at + step] = acc.astype(jnp.bfloat16).reshape(passes * ep_n, TILE, step)
 
     pl.semaphore_wait(barrier, ep_n + dp_n - 2)
 
-    def dispatch(off, carry):
-        target = flip(me, off, ep_n)
-        pltpu.make_async_remote_copy(
-            src_ref=disp.at[target],
-            dst_ref=rows.at[d * ep_n + me],
-            send_sem=disp_send,
-            recv_sem=disp_recv.at[me],
-            device_id={"dp": d, "ep": target},
-            device_id_type=MESH,
-        ).start()
-        return carry
-
-    lax.fori_loop(1, ep_n, dispatch, 0)
-    pltpu.make_async_copy(disp.at[me], rows.at[d * ep_n + me], disp_recv.at[me]).start()
-
-    def relay(off, carry):
-        source = flip(me, off, ep_n)
-        chunk = rows.at[d * ep_n + source]
-        drain(chunk, disp_recv.at[source])
-        for j in range(1, dp_n):
+    for turn in range(passes):
+
+        def dispatch(off, carry):
+            target = flip(me, off, ep_n)
             pltpu.make_async_remote_copy(
-                src_ref=chunk,
-                dst_ref=chunk,
-                send_sem=relay_send,
-                recv_sem=relay_recv.at[d],
-                device_id={"dp": lax.rem(d + j, jnp.int32(dp_n)), "ep": me},
+                src_ref=disp.at[turn * ep_n + target],
+                dst_ref=rows.at[turn * total + d * ep_n + me],
+                send_sem=disp_send,
+                recv_sem=disp_recv.at[turn * ep_n + me],
+                device_id={"dp": d, "ep": target},
                 device_id_type=MESH,
             ).start()
-        return carry
-
-    lax.fori_loop(0, ep_n, relay, 0)
+            return carry
+
+        lax.fori_loop(1, ep_n, dispatch, 0)
+        pltpu.make_async_copy(
+            disp.at[turn * ep_n + me],
+            rows.at[turn * total + d * ep_n + me],
+            disp_recv.at[turn * ep_n + me],
+        ).start()
+
+    def relay(turn, first, last):
+        def one(off, carry):
+            source = flip(me, off, ep_n)
+            chunk = rows.at[turn * total + d * ep_n + source]
+            drain(chunk, disp_recv.at[turn * ep_n + source])
+            for j in range(1, dp_n):
+                pltpu.make_async_remote_copy(
+                    src_ref=chunk,
+                    dst_ref=chunk,
+                    send_sem=relay_send,
+                    recv_sem=relay_recv.at[turn * dp_n + d],
+                    device_id={"dp": lax.rem(d + j, jnp.int32(dp_n)), "ep": me},
+                    device_id_type=MESH,
+                ).start()
+            return carry
+
+        lax.fori_loop(first, last, one, 0)
 
     unfold = fold_map((folds * group_rows, group * TILE), 0, group, cap)
     refold = fold_map((group * TILE, back_folds * group_rows), 1, group, cap)
 
-    loads[3].wait()
-    loads[4].wait()
-    for j in range(dp_n):
+    def first(turn, j):
         plane = lax.rem(d + j, jnp.int32(dp_n))
         if j > 0:
-            drain(rows.at[pl.ds(plane * ep_n, ep_n)], relay_recv.at[plane])
+            drain(rows.at[pl.ds(turn * total + plane * ep_n, ep_n)], relay_recv.at[turn * dp_n + plane])
         for g in range(ep_n // group):
-            tiles = rows[pl.ds(plane * ep_n + g * group, group)].reshape(group * TILE, fold_cols)
+            tiles = rows[pl.ds(turn * total + plane * ep_n + g * group, group)].reshape(group * TILE, fold_cols)
             flat = dot(unfold, tiles).astype(jnp.bfloat16)
             for f in range(folds):
                 xs[f, g * group_rows : (g + 1) * group_rows, :] = flat[
@@ -210,41 +216,42 @@
         acc = dot(xs[0], w1[:fold_cols, :])
         for f in range(1, folds):
             acc += dot(xs[f], w1[f * fold_cols : (f + 1) * fold_cols, :])
-        hid[plane * dp_n + d] = jax.nn.gelu(acc, approximate=True).astype(jnp.bfloat16)
+        hid[(turn * dp_n + plane) * dp_n + d] = jax.nn.gelu(acc, approximate=True).astype(jnp.bfloat16)
         for i in range(1, dp_n):
             pltpu.make_async_remote_copy(
-                src_ref=hid.at[plane * dp_n + d],
-                dst_ref=hid.at[plane * dp_n + d],
+                src_ref=hid.at[(turn * dp_n + plane) * dp_n + d],
+                dst_ref=hid.at[(turn * dp_n + plane) * dp_n + d],
                 send_sem=hid_send,
-                recv_sem=hid_recv.at[plane * dp_n + d],
+                recv_sem=hid_recv.at[(turn * dp_n + plane) * dp_n + d],
                 device_id={"dp": lax.rem(d + i, jnp.int32(dp_n)), "ep": me},
                 device_id_type=MESH,
             ).start()
 
     units = hid.shape[2]
-    for j in range(dp_n):
+
+    def second(turn, j):
         plane = lax.rem(d + j, jnp.int32(dp_n))
         for i in range(1, dp_n):
-            part = plane * dp_n + lax.rem(d + i, jnp.int32(dp_n))
+            part = (turn * dp_n + plane) * dp_n + lax.rem(d + i, jnp.int32(dp_n))
             drain(hid.at[part], hid_recv.at[part])
         for f in range(back_folds):
             cols = slice(f * back_cols, (f + 1) * back_cols)
-            acc = dot(hid[plane * dp_n], w2[:units, cols])
+            acc = dot(hid[(turn * dp_n + plane) * dp_n], w2[:units, cols])
             for i in range(1, dp_n):
-                acc += dot(hid[plane * dp_n + i], w2[i * units : (i + 1) * units, cols])
+                acc += dot(hid[(turn * dp_n + plane) * dp_n + i], w2[i * units : (i + 1) * units, cols])
             ys[f] = acc.astype(jnp.bfloat16)
         for g in range(ep_n // group):
             flat = jnp.concatenate(
                 [ys[f, g * group_rows : (g + 1) * group_rows, :] for f in range(back_folds)], axis=0
             )
             tiles = dot(refold, flat).astype(jnp.bfloat16)
-            back_out[pl.ds(plane * ep_n + g * group, group)] = tiles.reshape(group, TILE, back_cols)
+            back_out[pl.ds(turn * total + plane * ep_n + g * group, group)] = tiles.reshape(group, TILE, back_cols)
 
         def give_back(off, carry):
             target = flip(me, off, ep_n)
             pltpu.make_async_remote_copy(
-                src_ref=back_out.at[plane * ep_n + target],
-                dst_ref=back_in.at[d * ep_n + me],
+                src_ref=back_out.at[turn * total + plane * ep_n + target],
+                dst_ref=back_in.at[turn * total + d * ep_n + me],
                 send_sem=back_send,
                 recv_sem=back_recv,
                 device_id={"dp": plane, "ep": target},
@@ -255,14 +262,36 @@
         lax.fori_loop(1 if j == 0 else 0, ep_n, give_back, 0)
         if j == 0:
             pltpu.make_async_copy(
-                back_out.at[d * ep_n + me], back_in.at[d * ep_n + me], own_sem
+                back_out.at[turn * total + d * ep_n + me], back_in.at[turn * total + d * ep_n + me], own_sem
             ).start()
+
+    planes = range(dp_n)
+    relay(0, 0, ep_n)
+    loads[3].wait()
+    first(0, 0)
+    if passes > 1:
+        relay(1, 0, ep_n // 2)
+    for j in planes[1:]:
+        first(0, j)
+    if passes > 1:
+        relay(1, ep_n // 2, ep_n)
+        first(1, 0)
+    loads[4].wait()
+    second(0, 0)
+    if passes > 1:
+        for j in planes[1:]:
+            first(1, j)
+    for j in planes[1:]:
+        second(0, j)
+    if passes > 1:
+        for j in planes:
+            second(1, j)
 
     for load in loads[5:]:
         load.wait()
     attend(q, k, v, ck, cv, frames[0], attended)
 
-    col_at = iota((tokens, ep_n * TILE), 1)
+    col_at = iota((tokens, passes * ep_n * TILE), 1)
     picks = jnp.concatenate(
         [
             jnp.where(col_at - f * cap == place[c], 1.0, 0.0)
@@ -272,10 +301,13 @@
         axis=0,
     ).astype(jnp.bfloat16)
 
-    drain(back_in.at[pl.ds(0, total - 1)], back_recv)
-    drain(back_in.at[0], own_sem)
+    drain(back_in.at[pl.ds(0, passes * (total - 1))], back_recv)
+    drain(back_in.at[pl.ds(0, passes)], own_sem)
     for h in range(dp_n):
-        tiles = back_in[h * ep_n : (h + 1) * ep_n].reshape(ep_n * TILE, back_cols)
+        starts = [turn * total + h * ep_n for turn in range(passes)]
+        tiles = jnp.concatenate(
+            [back_in[at : at + ep_n].reshape(ep_n * TILE, back_cols) for at in starts], axis=0
+        )
         picked = dot(picks, tiles)
         for f in range(back_folds):
             at = 2 * f * tokens
@@ -284,11 +316,11 @@
                 gates[0] * picked[at : at + tokens] + gates[1] * picked[at + tokens : at + 2 * tokens]
             ).astype(jnp.bfloat16)
 
-    drain(disp.at[pl.ds(0, ep_n - 1)], disp_send)
+    drain(disp.at[pl.ds(0, passes * (ep_n - 1))], disp_send)
     if dp_n > 1:
-        drain(rows.at[pl.ds(0, (dp_n - 1) * ep_n)], relay_send)
-        drain(hid.at[pl.ds(0, dp_n * (dp_n - 1))], hid_send)
-    drain(back_out.at[pl.ds(0, total - 1)], back_send)
+        drain(rows.at[pl.ds(0, passes * (dp_n - 1) * ep_n)], relay_send)
+        drain(hid.at[pl.ds(0, passes * dp_n * (dp_n - 1))], hid_send)
+    drain(back_out.at[pl.ds(0, passes * (total - 1))], back_send)
 
 
 def shards(dp_n, ep_n, *args):
@@ -296,6 +328,8 @@
      queries, span_keys, span_values, cache_keys, cache_values, valid_frames) = args
     tokens, width = hidden_in.shape
     cap = max(2, 8 * tokens // (3 * ep_n))
+    passes = 2 if cap % 4 == 0 else 1
+    cap //= passes
     _, _, units = first_weight.shape
     _, all_units, cols = second_weight.shape
     folds = TILE // cap
@@ -311,7 +345,7 @@
         first_weight[0], second_weight[0],
     )
     return pl.pallas_call(
-        functools.partial(kernel, dp_n, ep_n, cap, back_folds),
+        functools.partial(kernel, dp_n, ep_n, passes, cap, back_folds),
         out_shape=(
             jax.ShapeDtypeStruct((tokens, width), bf16),
             jax.ShapeDtypeStruct(queries.shape, bf16),
@@ -329,20 +363,20 @@
             pltpu.VMEM(span_values.shape, bf16),
             pltpu.VMEM(cache_keys.shape[1:], bf16),
             pltpu.VMEM(cache_values.shape[1:], bf16),
-            pltpu.VMEM((ep_n, TILE, width // folds), bf16),
-            pltpu.VMEM((total, TILE, width // folds), bf16),
+            pltpu.VMEM((passes * ep_n, TILE, width // folds), bf16),
+            pltpu.VMEM((passes * total, TILE, width // folds), bf16),
             pltpu.VMEM((folds, slots, width // folds), bf16),
-            pltpu.VMEM((dp_n * dp_n, slots, units), bf16),
+            pltpu.VMEM((passes * dp_n * dp_n, slots, units), bf16),
             pltpu.VMEM((back_folds, slots, cols // back_folds), bf16),
-            pltpu.VMEM((total, TILE, cols // back_folds), bf16),
-            pltpu.VMEM((total, TILE, cols // back_folds), bf16),
+            pltpu.VMEM((passes * total, TILE, cols // back_folds), bf16),
+            pltpu.VMEM((passes * total, TILE, cols // back_folds), bf16),
             dma((len(streamed),)),
             dma(()),
-            dma((ep_n,)),
-            dma(()),
-            dma((dp_n,)),
-            dma(()),
-            dma((dp_n * dp_n,)),
+            dma((passes * ep_n,)),
+            dma(()),
+            dma((passes * dp_n,)),
+            dma(()),
+            dma((passes * dp_n * dp_n,)),
             dma(()),
             dma(()),
             dma(()),

time: 43.6 us -> 41.2 us (0.945)
  Pallas kernels: 40.8 us -> 38.4 us
    pallas_call x1, Pallas kernels: 40.8 us -> 38.4 us  [shards(): pl.pallas_call(functools.partial(kernel, dp_n, ep_n, passes, cap, back_fo...]
where the time goes in v3:
time: 41.2 us; the launch traced here: 41.1 us
  Pallas kernels  38.4 us (93%)
  local copies, waits for them, and re-layouts  1.32 us (3%)
  between operations  1.29 us (3%)
    pallas_call x1, Pallas kernels, shards(): pl.pallas_call(functools.partial(kernel, dp_n, ep_n, passes, cap, back_fo...  38.4 us
    unnamed x2, local copies, waits for them, and re-layouts  1.32 us

profile of v3, /device:TPU:0, one launch (start us, length us, event | category | flops | bytes accessed | tf_op | source)
XLA Modules:
  0.0 41.1 jit_solution(4179829746578346515)
XLA Ops:
  1.3 38.4 %shard_map.122 = (bf16[24,4096]{1,0:T(8,128)(2,1)S(1)}, bf16[24,2048]{1,0:T(8,128)(2,1)S(1)}) custom-call(s32[1]{0:T(128)S(6)} %copy.15.frames, s32[2,24]{1,0:T(2,128)} %bitcast.11, f32[16,24]{1,0:T(8,128)} %bitcast.10, bf16[24,4096]{1,0:T(8,128)(2,1)} %hidden_hbm.1, bf16[24,2048]{1,0:T(8,128)(2,1)} %q_hbm.1, bf16[24,2048]{1,0:T(8,128)(2,1)} %k_hbm.1, ...), custom_call_target="tpu_custom_call" | custom-call | tf_op jit(solution)/shard_map/pallas_call | solution.py:347
  39.7 0.7 %copy.16 = bf16[24,4096]{1,0:T(8,128)(2,1)} copy(bf16[24,4096]{1,0:T(8,128)(2,1)S(1)} %get-tuple-element.4) | data formatting | bytes 393216
  40.4 0.6 %copy.17 = bf16[24,2048]{1,0:T(8,128)(2,1)} copy(bf16[24,2048]{1,0:T(8,128)(2,1)S(1)} %get-tuple-element.5) | data formatting | bytes 196608
